TPU v7x, 32 devices: a whole 2x2x4 slice. The times are simulated.
32 devices in a mesh: dp: 4 (over x, core), ctx: 8 (over z, y).
Axes of the slice: x: 2, y: 2, z: 4, core: 2. Of those that a mesh axis runs over, the one named last changes fastest.
Arguments:
- density: float32 [128, 64, 64], P(('dp', 'ctx')), parts along dimension 0, may hold values from 0.1 to 50, as said below
- stem_weight: bfloat16 [216, 1024], replicated, may hold values from -0.4375 to 0.4375
- stem_bias: float32 [1024], replicated, may hold values from -3 to 3
- pos_embed: bfloat16 [2048, 1024], P('ctx'), may hold values from -3 to 3
- ln1_gain: float32 [1024], replicated, may hold values from 0.25 to 1.75
- ln1_bias: float32 [1024], replicated, may hold values from -2 to 2
- w_qkv: bfloat16 [1024, 3072], replicated, may hold values from -2 to 2
- qkv_bias: float32 [3072], replicated, may hold values from -2 to 2
- w_out: bfloat16 [1024, 1024], replicated, may hold values from -0.1875 to 0.1875
- out_bias: float32 [1024], replicated, may hold values from -2 to 2
- ln2_gain: float32 [1024], replicated, may hold values from 0.25 to 1.75
- ln2_bias: float32 [1024], replicated, may hold values from -2 to 2
- w_fc1: bfloat16 [1024, 4096], replicated, may hold values from -0.1875 to 0.1875
- fc1_bias: float32 [4096], replicated, may hold values from -3 to 3
- w_fc2: bfloat16 [4096, 1024], replicated, may hold values from -0.09375 to 0.09375
- fc2_bias: float32 [1024], replicated, may hold values from -2 to 2
Outputs:
- encoded: bfloat16 [8192, 1024], P(('dp', 'ctx')), parts along dimension 0
There are 4 independent parts, one for each index of `dp`. A program takes and returns all parts, laid end to end along the dimension named above; an argument that names none is the same for every part. Nothing has to cross between parts.
Inputs may be any that keep to these rules, and one draw needn't show every extreme that they name: density is positive.
All inputs are finite; a program needn't handle non-finite values.
Results may differ from a plain program's by a relative error of at most 0.013.
Values may be sent and summed in bfloat16 or wider, within the bound.
A program may use at most 384 MiB of HBM per device.

v0:
```python
import functools
import math

import jax
import jax.numpy as jnp
from jax import lax
from jax.experimental import pallas as pl
from jax.experimental.pallas import tpu as pltpu
from jax.sharding import PartitionSpec as P

HEADS = 16
KERNEL = 6
STRIDE = 4
MESH = pl.DeviceIdType.MESH
F32 = jnp.float32
BF16 = jnp.bfloat16


def iota(shape, axis):
    return lax.broadcasted_iota(jnp.int32, shape, axis)


def norm_rows(values, gain_vector, shift_vector):
    center = values - jnp.mean(values, axis=-1, keepdims=True)
    spread = jnp.mean(center * center, axis=-1, keepdims=True)
    return center * lax.rsqrt(spread + 1e-06) * gain_vector + shift_vector


def layer_kernel(
    n,
    cells,
    density,
    stem_weight,
    stem_bias,
    pos_embed,
    ln1_gain,
    ln1_bias,
    w_qkv_hbm,
    qkv_bias,
    w_out_hbm,
    out_bias,
    ln2_gain,
    ln2_bias,
    w_fc1_hbm,
    fc1_bias,
    w_fc2_hbm,
    fc2_bias,
    encoded,
    w_qkv,
    w_out,
    w_fc1,
    w_fc2,
    weight_sem,
    halo,
    sum_send,
    sum_got,
    edge_send_sem,
    edge_recv_sem,
    sum_send_sem,
    sum_recv_sem,
    select_rows,
    fold,
    planes_wide,
    kernel_rows,
    residual,
    normed,
    outgoing,
    query_got,
    key_got,
    value_got,
    value_wide,
    mixed_send,
    mixed_got,
    attended,
    total,
    send_sem,
    recv_sem,
):
    me = lax.axis_index("ctx")
    planes, side, _ = density.shape
    tokens, width = residual.shape
    head_size = width // HEADS
    local_heads = max(HEADS // n, 1)
    groups = max(n // HEADS, 1)
    group_width = local_heads * head_size
    share = tokens // groups
    grid = side // STRIDE
    window = planes + 2

    weights = [
        pltpu.make_async_copy(source, target, weight_sem.at[i])
        for i, (source, target) in enumerate(
            ((w_qkv_hbm, w_qkv), (w_out_hbm, w_out), (w_fc1_hbm, w_fc1), (w_fc2_hbm, w_fc2))
        )
    ]
    for copy in weights:
        copy.start()

    barrier = pltpu.get_barrier_semaphore()

    def each_peer(action):
        def step(offset, carry):
            action(lax.rem(me + offset, n))
            return carry

        lax.fori_loop(1, n, step, 0)

    each_peer(
        lambda peer: pl.semaphore_signal(
            barrier, inc=1, device_id={"ctx": peer}, device_id_type=MESH
        )
    )

    own = jnp.sum(density[...], axis=0)
    own = jnp.sum(own, axis=(0, 1), keepdims=True)
    sum_send[...] = jnp.broadcast_to(own, sum_send.shape)
    sum_got[me] = jnp.broadcast_to(own, sum_send.shape)

    @pl.when(me == 0)
    def _():
        halo[0] = jnp.ones((side, side), F32)

    @pl.when(me == n - 1)
    def _():
        halo[1] = jnp.ones((side, side), F32)

    pl.semaphore_wait(barrier, n - 1)

    def edge(side_index, plane, peer):
        return pltpu.make_async_remote_copy(
            src_ref=density.at[plane],
            dst_ref=halo.at[side_index],
            send_sem=edge_send_sem.at[side_index],
            recv_sem=edge_recv_sem.at[side_index],
            device_id={"ctx": peer},
            device_id_type=MESH,
        )

    up = edge(0, planes - 1, lax.rem(me + 1, n))
    down = edge(1, 0, lax.rem(me + n - 1, n))

    def sum_copy(source, peer):
        return pltpu.make_async_remote_copy(
            src_ref=sum_send,
            dst_ref=sum_got.at[source],
            send_sem=sum_send_sem.at[peer],
            recv_sem=sum_recv_sem.at[source],
            device_id={"ctx": peer},
            device_id_type=MESH,
        )

    each_peer(lambda peer: sum_copy(me, peer).start())

    @pl.when(me < n - 1)
    def _():
        up.start()

    @pl.when(me > 0)
    def _():
        down.start()

    pair = 2 * side
    row = iota((tokens, side), 0)
    col = iota((tokens, side), 1)
    for b in range(KERNEL):
        hit = col == STRIDE * (row // grid) - 1 + b
        select_rows[b] = jnp.where(hit, 1.0, 0.0).astype(BF16)
    lane_row = iota((pair, 256), 0)
    lane_col = iota((pair, 256), 1)
    high = lane_row // side
    offset_c = ((lane_row + 1) & (STRIDE - 1)) + STRIDE * high
    for b in range(KERNEL):
        for a in range(window):
            hit = (offset_c < KERNEL) & (lane_col == (a * KERNEL + b) * KERNEL + offset_c)
            fold[b, a * pair : (a + 1) * pair, :] = jnp.where(hit, 1.0, 0.0).astype(BF16)
    taps = stem_weight.shape[0]
    kernel_rows[...] = jnp.zeros(kernel_rows.shape, BF16)
    kernel_rows[0:taps, :] = stem_weight[...]
    tile_row = iota((tokens, pair), 0)
    tile_lane = iota((tokens, pair), 1)
    keep = (((tile_lane & (side - 1)) + 1) // STRIDE - tile_lane // side) == (
        tile_row & (grid - 1)
    )
    keep = jnp.where(keep, 1.0, 0.0).astype(BF16)

    each_peer(lambda peer: sum_copy(peer, peer).wait_recv())

    @pl.when(me > 0)
    def _():
        up.wait_recv()

    @pl.when(me < n - 1)
    def _():
        down.wait_recv()

    mean_density = (jnp.sum(sum_got[...], axis=0)[0:1, 0:1]) / cells
    for a in range(window):
        if a == 0:
            plane = jnp.where(me > 0, jnp.log(halo[0] / mean_density), 0.0)
        elif a == window - 1:
            plane = jnp.where(me < n - 1, jnp.log(halo[1] / mean_density), 0.0)
        else:
            plane = jnp.log(density[a - 1] / mean_density)
        plane = plane.astype(BF16)
        planes_wide[:, a * pair : (a + 1) * pair] = jnp.concatenate([plane, plane], axis=1)

    keep_wide = jnp.concatenate([keep] * window, axis=1)
    patches = jnp.zeros((tokens, 256), F32)
    for b in range(KERNEL):
        rows = jnp.dot(select_rows[b], planes_wide[...], preferred_element_type=F32)
        rows = rows.astype(BF16) * keep_wide
        patches += jnp.dot(rows, fold[b], preferred_element_type=F32)
    embedded = jnp.dot(patches.astype(BF16), kernel_rows[...], preferred_element_type=F32)
    embedded = embedded + stem_bias[...] + pos_embed[...].astype(F32)
    residual[...] = embedded.astype(BF16)
    normed[...] = norm_rows(residual[...].astype(F32), ln1_gain[...], ln1_bias[...]).astype(BF16)

    def head_group(peer):
        return peer // groups

    def my_rows(peer):
        return pl.ds(pl.multiple_of(lax.rem(peer, groups) * share, share), share)

    def projected_copy(kind, source, peer):
        piece = outgoing.at[kind, head_group(peer)]
        got = (query_got, key_got, value_got)[kind]
        if kind == 0:
            piece = piece.at[my_rows(peer)]
        return pltpu.make_async_remote_copy(
            src_ref=piece,
            dst_ref=got.at[source],
            send_sem=send_sem.at[kind, peer],
            recv_sem=recv_sem.at[kind, source],
            device_id={"ctx": peer},
            device_id_type=MESH,
        )

    weights[0].wait()
    block = 256
    for kind in (1, 2, 0):
        for start in range(0, width, block):
            columns = slice(kind * width + start, kind * width + start + block)
            result = jnp.dot(normed[...], w_qkv[:, columns], preferred_element_type=F32)
            result = result + qkv_bias[:, columns]
            if kind == 0:
                result = result * (1.0 / head_size**0.5)
            result = result.astype(BF16)
            for part in range(block // group_width):
                outgoing[kind, start // group_width + part] = result[
                    :, part * group_width : (part + 1) * group_width
                ]
        each_peer(lambda peer: projected_copy(kind, me, peer).start())
    query_got[me] = outgoing[0, head_group(me), my_rows(me), :]
    key_got[me] = outgoing[1, head_group(me)]
    value_got[me] = outgoing[2, head_group(me)]

    each_peer(lambda peer: projected_copy(1, peer, peer).wait_recv())
    each_peer(lambda peer: projected_copy(2, peer, peer).wait_recv())

    keys_total = n * tokens
    wide = group_width % 128 == 0
    if wide:
        value_wide[:, 0:group_width] = value_got[...].reshape(keys_total, group_width)
        value_wide[:, group_width:] = jnp.ones((keys_total, group_width), BF16)

    def mixed_copy(source, peer):
        return pltpu.make_async_remote_copy(
            src_ref=mixed_send.at[peer],
            dst_ref=mixed_got.at[source],
            send_sem=send_sem.at[3, peer],
            recv_sem=recv_sem.at[3, source],
            device_id={"ctx": peer},
            device_id_type=MESH,
        )

    def attend(offset, carry):
        peer = lax.rem(me + n - offset, n)

        @pl.when(offset > 0)
        def _():
            projected_copy(0, peer, peer).wait_recv()

        query = query_got[peer]
        lane = iota((share, group_width), 1) // head_size
        mixed = None
        for head in range(local_heads):
            mine = query if local_heads == 1 else jnp.where(lane == head, query, jnp.zeros_like(query))
            scores = lax.dot_general(
                mine,
                key_got[...].reshape(keys_total, group_width),
                (((1,), (1,)), ((), ())),
                preferred_element_type=F32,
            )
            weight = jnp.exp(scores - jnp.max(scores, axis=1, keepdims=True))
            if wide:
                product = jnp.dot(weight.astype(BF16), value_wide[...], preferred_element_type=F32)
                part = product[:, 0:group_width] / product[:, group_width:]
            else:
                product = jnp.dot(
                    weight.astype(BF16),
                    value_got[...].reshape(keys_total, group_width),
                    preferred_element_type=F32,
                )
                part = product / jnp.sum(weight, axis=1, keepdims=True)
            mixed = part if mixed is None else jnp.where(lane == head, part, mixed)
        mixed_send[peer] = mixed.astype(BF16)

        @pl.when(offset > 0)
        def _():
            mixed_copy(me, peer).start()

        @pl.when(offset == 0)
        def _():
            mixed_got[me] = mixed.astype(BF16)

        return carry

    lax.fori_loop(0, n, attend, 0)

    each_peer(lambda peer: mixed_copy(peer, peer).wait_recv())
    for piece in range(n):
        first = (piece % groups) * share
        column = (piece // groups) * group_width
        attended[first : first + share, column : column + group_width] = mixed_got[piece]

    weights[1].wait()
    stream = (
        residual[...].astype(F32)
        + jnp.dot(attended[...], w_out[...], preferred_element_type=F32)
        + out_bias[...]
    ).astype(BF16)
    residual[...] = stream
    stream = stream.astype(F32)
    normed[...] = norm_rows(stream, ln2_gain[...], ln2_bias[...]).astype(BF16)
    total[...] = stream + fc2_bias[...]

    weights[2].wait()
    weights[3].wait()
    hidden_width = w_fc1.shape[1]
    tile = math.gcd(hidden_width, 512)
    for start in range(0, hidden_width, tile):
        columns = slice(start, start + tile)
        hidden = jnp.dot(normed[...], w_fc1[:, columns], preferred_element_type=F32)
        hidden = hidden + fc1_bias[:, columns]
        hidden = 0.5 * hidden * (1.0 + lax.erf(hidden * math.sqrt(0.5)))
        total[...] += jnp.dot(hidden.astype(BF16), w_fc2[columns, :], preferred_element_type=F32)
    encoded[...] = total[...].astype(BF16)

    def finish(peer):
        sum_copy(me, peer).wait_send()
        for kind in range(3):
            projected_copy(kind, me, peer).wait_send()
        mixed_copy(me, peer).wait_send()

    each_peer(finish)

    @pl.when(me < n - 1)
    def _():
        up.wait_send()

    @pl.when(me > 0)
    def _():
        down.wait_send()


def per_device(
    density,
    stem_weight,
    stem_bias,
    pos_embed,
    ln1_gain,
    ln1_bias,
    w_qkv,
    qkv_bias,
    w_out,
    out_bias,
    ln2_gain,
    ln2_bias,
    w_fc1,
    fc1_bias,
    w_fc2,
    fc2_bias,
):
    n = lax.axis_size("ctx")
    tokens, width = pos_embed.shape
    hidden_width = w_fc1.shape[1]
    planes, side, _ = density.shape
    assert planes == STRIDE and tokens == (side // STRIDE) ** 2
    head_size = width // HEADS
    local_heads = max(HEADS // n, 1)
    groups = max(n // HEADS, 1)
    head_groups = HEADS // local_heads
    group_width = local_heads * head_size
    share = tokens // groups
    pair = 2 * side
    window = planes + 2
    vmem = pl.BlockSpec(memory_space=pltpu.VMEM)
    hbm = pl.BlockSpec(memory_space=pl.ANY)

    def line(vector):
        return vector.reshape(1, -1)

    dma = pltpu.SemaphoreType.DMA
    wide_shape = (n * tokens, 2 * group_width) if group_width % 128 == 0 else (16, 128)
    return pl.pallas_call(
        functools.partial(layer_kernel, n, density.size * n),
        out_shape=jax.ShapeDtypeStruct((tokens, width), BF16),
        in_specs=[
            vmem, vmem, vmem, vmem, vmem, vmem, hbm, vmem,
            hbm, vmem, vmem, vmem, hbm, vmem, hbm, vmem,
        ],
        out_specs=vmem,
        scratch_shapes=[
            pltpu.VMEM(w_qkv.shape, BF16),
            pltpu.VMEM(w_out.shape, BF16),
            pltpu.VMEM(w_fc1.shape, BF16),
            pltpu.VMEM(w_fc2.shape, BF16),
            dma((4,)),
            pltpu.VMEM((2, side, side), F32),
            pltpu.VMEM((8, 128), F32),
            pltpu.VMEM((n, 8, 128), F32),
            dma((2,)),
            dma((2,)),
            dma((n,)),
            dma((n,)),
            pltpu.VMEM((KERNEL, tokens, side), BF16),
            pltpu.VMEM((KERNEL, window * pair, 256), BF16),
            pltpu.VMEM((side, window * pair), BF16),
            pltpu.VMEM((256, width), BF16),
            pltpu.VMEM((tokens, width), BF16),
            pltpu.VMEM((tokens, width), BF16),
            pltpu.VMEM((3, head_groups, tokens, group_width), BF16),
            pltpu.VMEM((n, share, group_width), BF16),
            pltpu.VMEM((n, tokens, group_width), BF16),
            pltpu.VMEM((n, tokens, group_width), BF16),
            pltpu.VMEM(wide_shape, BF16),
            pltpu.VMEM((n, share, group_width), BF16),
            pltpu.VMEM((n, share, group_width), BF16),
            pltpu.VMEM((tokens, width), BF16),
            pltpu.VMEM((tokens, width), F32),
            dma((4, n)),
            dma((4, n)),
        ],
        compiler_params=pltpu.CompilerParams(
            collective_id=0, has_side_effects=True, vmem_limit_bytes=60 * 1024 * 1024
        ),
    )(
        density,
        stem_weight,
        line(stem_bias),
        pos_embed,
        line(ln1_gain),
        line(ln1_bias),
        w_qkv,
        line(qkv_bias),
        w_out,
        line(out_bias),
        line(ln2_gain),
        line(ln2_bias),
        w_fc1,
        line(fc1_bias),
        w_fc2,
        line(fc2_bias),
    )


def solution(mesh):
    in_specs = (P(("dp", "ctx"), None, None), P(), P(), P("ctx", None)) + (P(),) * 12
    return jax.shard_map(
        per_device,
        mesh=mesh,
        in_specs=in_specs,
        out_specs=P(("dp", "ctx"), None),
        check_vma=False,
    )
```

profile of v0, /device:TPU:0, one launch (start us, length us, event | category | flops | bytes accessed | tf_op | source)
XLA Modules:
  0.0 77.0 jit_solution(8509625443887957677)
XLA Ops:
  0.0 75.1 %shard_map.154 = bf16[256,1024]{1,0:T(8,128)(2,1)} custom-call(f32[4,64,64]{2,1,0:T(8,128)} %density.1, bf16[216,1024]{1,0:T(8,128)(2,1)} %stem_weight.1, f32[1,1024]{1,0:T(1,128)} %bitcast.11, bf16[256,1024]{1,0:T(8,128)(2,1)} %pos_embed.1, f32[1,1024]{1,0:T(1,128)} %bitcast.12, f32[1,1024]{1,0:T(1,128)} %bitcast.13, bf16[1024,3072]{1,0:T(8,128)(2,1)} %w_qkv_hbm.1, ...), custom_call_target="tpu_custom_call" | custom-call | tf_op jit(solution)/shard_map/pallas_call | solution.py:405
  75.1 1.9 %copy.18 = bf16[256,1024]{1,0:T(8,128)(2,1)} copy(bf16[256,1024]{1,0:T(8,128)(2,1)} %shard_map.154) | data formatting | bytes 1048576
where the time goes:
time: 77.2 us; the launch traced here: 77 us
  Pallas kernels  75.1 us (97%)
  local copies, waits for them, and re-layouts  1.87 us (2%)
    pallas_call x1, Pallas kernels, per_device(): pl.pallas_call(functools.partial(layer_kernel, n, density.size * n), out_...  75.1 us
    unnamed x1, local copies, waits for them, and re-layouts  1.87 us

commit v1 on v0

--- a/solution.py
+++ b/solution.py
@@ -11,6 +11,7 @@
 HEADS = 16
 KERNEL = 6
 STRIDE = 4
+ROWS = 128
 MESH = pl.DeviceIdType.MESH
 F32 = jnp.float32
 BF16 = jnp.bfloat16
@@ -18,6 +19,14 @@
 
 def iota(shape, axis):
     return lax.broadcasted_iota(jnp.int32, shape, axis)
+
+
+def partner(me, mask, n):
+    result, bit = 0, 1
+    while bit < n:
+        result += ((me // bit + mask // bit) % 2) * bit
+        bit *= 2
+    return result
 
 
 def norm_rows(values, gain_vector, shift_vector):
@@ -100,7 +109,7 @@
 
     def each_peer(action):
         def step(offset, carry):
-            action(lax.rem(me + offset, n))
+            action(partner(me, n - offset, n))
             return carry
 
         lax.fori_loop(1, n, step, 0)
@@ -274,36 +283,36 @@
         )
 
     def attend(offset, carry):
-        peer = lax.rem(me + n - offset, n)
+        peer = partner(me, lax.rem(n - offset, n), n)
 
         @pl.when(offset > 0)
         def _():
             projected_copy(0, peer, peer).wait_recv()
 
-        query = query_got[peer]
-        lane = iota((share, group_width), 1) // head_size
-        mixed = None
-        for head in range(local_heads):
-            mine = query if local_heads == 1 else jnp.where(lane == head, query, jnp.zeros_like(query))
-            scores = lax.dot_general(
-                mine,
-                key_got[...].reshape(keys_total, group_width),
-                (((1,), (1,)), ((), ())),
-                preferred_element_type=F32,
-            )
-            weight = jnp.exp(scores - jnp.max(scores, axis=1, keepdims=True))
-            if wide:
-                product = jnp.dot(weight.astype(BF16), value_wide[...], preferred_element_type=F32)
-                part = product[:, 0:group_width] / product[:, group_width:]
-            else:
-                product = jnp.dot(
-                    weight.astype(BF16),
-                    value_got[...].reshape(keys_total, group_width),
+        rows = min(share, ROWS)
+        for first in range(0, share, rows):
+            query = query_got[peer, first : first + rows, :]
+            lane = iota((rows, group_width), 1) // head_size
+            mixed = None
+            for head in range(local_heads):
+                mine = query
+                if local_heads > 1:
+                    mine = jnp.where(lane == head, query, jnp.zeros_like(query))
+                scores = lax.dot_general(
+                    mine,
+                    key_got[...].reshape(keys_total, group_width),
+                    (((1,), (1,)), ((), ())),
                     preferred_element_type=F32,
                 )
-                part = product / jnp.sum(weight, axis=1, keepdims=True)
-            mixed = part if mixed is None else jnp.where(lane == head, part, mixed)
-        mixed_send[peer] = mixed.astype(BF16)
+                weight = jnp.exp(scores - jnp.max(scores, axis=1, keepdims=True))
+                values = value_wide[...] if wide else value_got[...].reshape(keys_total, group_width)
+                product = jnp.dot(weight.astype(BF16), values, preferred_element_type=F32)
+                if wide:
+                    part = product[:, 0:group_width] / product[:, group_width:]
+                else:
+                    part = product / jnp.sum(weight, axis=1, keepdims=True)
+                mixed = part if mixed is None else jnp.where(lane == head, part, mixed)
+            mixed_send[peer, first : first + rows, :] = mixed.astype(BF16)
 
         @pl.when(offset > 0)
         def _():
@@ -311,7 +320,7 @@
 
         @pl.when(offset == 0)
         def _():
-            mixed_got[me] = mixed.astype(BF16)
+            mixed_got[me] = mixed_send[me]
 
         return carry
 

time: 77.2 us -> 72.4 us (0.938)
  Pallas kernels: 75.1 us -> 70.4 us
    pallas_call x1, Pallas kernels: 75.1 us -> 70.4 us  [per_device(): pl.pallas_call(functools.partial(layer_kernel, n, density.size * n), out_...]
where the time goes in v1:
time: 72.4 us; the launch traced here: 72.2 us
  Pallas kernels  70.4 us (97%)
  local copies, waits for them, and re-layouts  1.87 us (3%)
    pallas_call x1, Pallas kernels, per_device(): pl.pallas_call(functools.partial(layer_kernel, n, density.size * n), out_...  70.4 us
    unnamed x1, local copies, waits for them, and re-layouts  1.87 us

profile of v1, /device:TPU:0, one launch (start us, length us, event | category | flops | bytes accessed | tf_op | source)
XLA Modules:
  0.0 72.2 jit_solution(5199820490417347258)
XLA Ops:
  0.0 70.4 %shard_map.154 = bf16[256,1024]{1,0:T(8,128)(2,1)} custom-call(f32[4,64,64]{2,1,0:T(8,128)} %density.1, bf16[216,1024]{1,0:T(8,128)(2,1)} %stem_weight.1, f32[1,1024]{1,0:T(1,128)} %bitcast.11, bf16[256,1024]{1,0:T(8,128)(2,1)} %pos_embed.1, f32[1,1024]{1,0:T(1,128)} %bitcast.12, f32[1,1024]{1,0:T(1,128)} %bitcast.13, bf16[1024,3072]{1,0:T(8,128)(2,1)} %w_qkv_hbm.1, ...), custom_call_target="tpu_custom_call" | custom-call | tf_op jit(solution)/shard_map/pallas_call | solution.py:414
  70.4 1.9 %copy.18 = bf16[256,1024]{1,0:T(8,128)(2,1)} copy(bf16[256,1024]{1,0:T(8,128)(2,1)} %shard_map.154) | data formatting | bytes 1048576
